TPU v7x, 256 devices: a whole 4x4x8 slice. The times are simulated.
256 devices in a mesh: band: 8 (over z_lo, core), lane: 32 (over z_hi, y, x).
Axes of the slice: x: 4, y: 4, z: 8 (z_hi: 2, z_lo: 4; z = z_hi * 4 + z_lo), core: 2. Of those that a mesh axis runs over, the one named last changes fastest.
Arguments:
- load_terms: float32 [512, 2048, 128], P('band', 'lane'), may hold values from -6 to 6
- start_values: float32 [512, 2048, 128], P('band', 'lane'), may hold values from -6 to 6
- reaction_rate: float32 [512, 2048, 128], P('band', 'lane'), may hold values from 0.1 to 0.9
Outputs:
- solution: float32 [512, 2048, 128], P('band', 'lane')
All inputs are finite; a program needn't handle non-finite values.
Results may differ from a plain program's by a relative error of at most 0.0003.
Values sent between devices are 32-bit elements.
No kernel may reach another device: no remote copies, remote signals or barrier semaphores. Data moves between devices by JAX's collectives and lax.ppermute only.
A program may use at most 64 MiB of HBM per device.

v0:
```python
import jax
import jax.numpy as jnp
from jax import lax
from jax.experimental import pallas as pl
from jax.experimental.pallas import tpu as pltpu
from jax.sharding import PartitionSpec as P

RATIO = 4
BEFORE = 3
AFTER = 2
INNER = 13

N = 64
C = N // RATIO
L = 128
DS = BEFORE + AFTER
DF = DS - 1
DEPTH = DS + 2 * DF
R0 = DS
C0 = 8
ROWS = N + 2 * DS
COLS = N + 16
H = INNER
CR = C + 2 * H
CC0 = 16
CCOLS = 48
WIDTHS = [C + 2 * (H + 1 - j) for j in range(1, H + 1)]
STARTS = [sum(WIDTHS[:k]) for k in range(H)]
BANDMSG = -(-sum(WIDTHS) // 8) * 8
FIT = 16 * 2**20

f32 = jnp.float32


def parity(axis):
    return lax.rem(lax.axis_index(axis), 2) == 0


def sds(*shape):
    return jax.ShapeDtypeStruct(shape, f32)


VM = pl.BlockSpec(memory_space=pltpu.VMEM)
ANY = pl.BlockSpec(memory_space=pl.ANY)


def call(body, outs, ins, scratch=(), out_specs=None, aliases=None, flops=10**6, name=None, inner=True):
    return pl.pallas_call(
        body,
        out_shape=[pltpu.VMEM(o.shape, o.dtype) for o in outs] if inner else outs,
        in_specs=ins,
        out_specs=out_specs if out_specs is not None else [VM] * len(outs),
        scratch_shapes=list(scratch),
        input_output_aliases=aliases or {},
        compiler_params=pltpu.CompilerParams(vmem_limit_bytes=FIT),
        cost_estimate=pl.CostEstimate(flops=flops, bytes_accessed=8 * 10**6, transcendentals=0),
        name=name,
    )


def pack_fine(load, start, mass, m_even, m_odd, b_even, b_odd, side, sem_side, sem_band):
    copies = []
    for k, src in enumerate((start, load, mass)):
        for s, at in enumerate((0, N - 8)):
            copies.append(
                pltpu.make_async_copy(src.at[:, pl.ds(at, 8)], side.at[k, s], sem_side.at[k, s])
            )
    even = parity("band")
    bands = []
    for which, (dst, bottom) in enumerate(((b_even, even), (b_odd, jnp.logical_not(even)))):
        at = 0
        for k, (src, depth) in enumerate(((start, DS), (load, DF), (mass, DF))):
            first = jnp.where(bottom, N - depth, 0)
            bands.append(
                pltpu.make_async_copy(
                    src.at[pl.ds(first, depth)], dst.at[pl.ds(at, depth)], sem_band.at[which, k]
                )
            )
            at += depth
    for c in copies:
        c.start()
    for c in bands:
        c.start()
    for c in copies:
        c.wait()

    def pack(dst, s):
        def group(g, carry):
            base = pl.multiple_of(g * (8 * DEPTH), 8)
            for r in range(8):
                at = r * DEPTH
                for k, depth in enumerate((DS, DF, DF)):
                    lo = 0 if s == 0 else 8 - depth
                    dst[pl.ds(base + at, depth), :] = side[k, s, g * 8 + r, lo : lo + depth, :]
                    at += depth
            return carry

        lax.fori_loop(0, N // 8, group, 0)

    lane_even = parity("lane")

    @pl.when(lane_even)
    def _():
        pack(m_even, 1)
        pack(m_odd, 0)

    @pl.when(jnp.logical_not(lane_even))
    def _():
        pack(m_even, 0)
        pack(m_odd, 1)

    for c in bands:
        c.wait()


def pack_corners(m_even, m_odd, c_even, c_odd):
    rows = DF * DEPTH

    def fill(left, right):
        def put(dst, first):
            dst[0:rows, :] = left[first : first + rows, :]
            dst[rows : 2 * rows, :] = right[first : first + rows, :]

        even = parity("band")

        @pl.when(even)
        def _():
            put(c_even, (N - DF) * DEPTH)
            put(c_odd, 0)

        @pl.when(jnp.logical_not(even))
        def _():
            put(c_even, 0)
            put(c_odd, (N - DF) * DEPTH)

    lane_even = parity("lane")

    @pl.when(lane_even)
    def _():
        fill(m_odd, m_even)

    @pl.when(jnp.logical_not(lane_even))
    def _():
        fill(m_even, m_odd)


def pack_coarse_lanes(own, m_even, m_odd):
    def put(right, left):
        for i in range(C):
            row = own(i)
            right[i * H : (i + 1) * H, :] = row[C - H :, :]
            left[i * H : (i + 1) * H, :] = row[:H, :]

    even = parity("lane")

    @pl.when(even)
    def _():
        put(m_even, m_odd)

    @pl.when(jnp.logical_not(even))
    def _():
        put(m_odd, m_even)


def place_coarse_lanes(ext, m_even, m_odd):
    def put(left, right):
        for i in range(C):
            ext[H + i, CC0 - H : CC0, :] = left[i * H : (i + 1) * H, :]
            ext[H + i, CC0 + C : CC0 + C + H, :] = right[i * H : (i + 1) * H, :]

    even = parity("lane")

    @pl.when(even)
    def _():
        put(m_odd, m_even)

    @pl.when(jnp.logical_not(even))
    def _():
        put(m_even, m_odd)


def pack_coarse_bands(ext, b_even, b_odd):
    def put(down, up):
        for j in range(1, H + 1):
            reach, at, wide = H + 1 - j, STARTS[j - 1], WIDTHS[j - 1]
            cols = slice(CC0 - reach, CC0 + C + reach)
            down[at : at + wide, :] = ext[H + C - j, cols, :]
            up[at : at + wide, :] = ext[H + j - 1, cols, :]
        for dst in (down, up):
            dst[sum(WIDTHS) :, :] = jnp.zeros((BANDMSG - sum(WIDTHS), L), f32)

    even = parity("band")

    @pl.when(even)
    def _():
        put(b_even, b_odd)

    @pl.when(jnp.logical_not(even))
    def _():
        put(b_odd, b_even)


def place_coarse_bands(ext, b_even, b_odd):
    def put(above, below):
        for j in range(1, H + 1):
            reach, at, wide = H + 1 - j, STARTS[j - 1], WIDTHS[j - 1]
            cols = slice(CC0 - reach, CC0 + C + reach)
            ext[H - j, cols, :] = above[at : at + wide, :]
            ext[H + C + j - 1, cols, :] = below[at : at + wide, :]

    even = parity("band")

    @pl.when(even)
    def _():
        put(b_odd, b_even)

    @pl.when(jnp.logical_not(even))
    def _():
        put(b_even, b_odd)


def weight(mass):
    return 0.8 / (4.0 + mass)


def sweep_rows(src, dst, w, f, first, last, segments, per=2):
    def one(r):
        for lo, hi in segments:
            around = (
                (src[r - 1, lo:hi, :] + src[r + 1, lo:hi, :])
                + (src[r, lo - 1 : hi - 1, :] + src[r, lo + 1 : hi + 1, :])
                + f[r, lo:hi, :]
            )
            dst[r, lo:hi, :] = 0.2 * src[r, lo:hi, :] + w[r, lo:hi, :] * around

    whole = (last - first) // per

    def group(g, carry):
        for k in range(per):
            one(first + g * per + k)
        return carry

    lax.fori_loop(0, whole, group, 0)
    for r in range(first + whole * per, last):
        one(r)


def gather_columns(line, row):
    line[...] = row
    total = line[pl.ds(0, C, stride=RATIO), :]
    for k in range(1, RATIO):
        total = total + line[pl.ds(k, C, stride=RATIO), :]
    return total * (1.0 / RATIO)


def prepare(load, start, mass, u, f, w, a4, cm, m_even, m_odd, line, sems):
    own = (pl.ds(R0, N), pl.ds(C0, N))
    copies = [
        pltpu.make_async_copy(mass, a4, sems.at[0]),
        pltpu.make_async_copy(load, f.at[own], sems.at[1]),
        pltpu.make_async_copy(start, u.at[own], sems.at[2]),
    ]
    for c in copies:
        c.start()
    copies[0].wait()

    def block(i, carry):
        total = jnp.zeros((N, L), f32)
        for k in range(RATIO):
            r = i * RATIO + k
            m = a4[r]
            total = total + m
            a = 4.0 + m
            a4[r] = a
            w[R0 + r, C0 : C0 + N, :] = 0.8 / a
        cm[i] = gather_columns(line, total)
        return carry

    lax.fori_loop(0, C, block, 0)
    pack_coarse_lanes(lambda i: cm[i], m_even, m_odd)
    for c in copies[1:]:
        c.wait()


FINE_SEGMENTS = ((C0 - DF, C0), (C0, C0 + N), (C0 + N, C0 + N + DF))


def before(u_in, f_in, w_in, a4, cm, re, ro, be, bo, ce, co, mre, mro, v, f, w, mext, l_even, l_odd, mb_even, mb_odd, cl, u, line):
    def rows_copy(g, carry):
        for k in range(2):
            r = R0 + 2 * g + k
            u[r, C0 : C0 + N, :] = u_in[r, C0 : C0 + N, :]
        return carry

    lax.fori_loop(0, N // 2, rows_copy, 0)
    R1, C1 = R0 + N, C0 + N

    def put_left(r, msg, at):
        u[r, C0 - DS : C0, :] = msg[at : at + DS, :]
        f[r, C0 - DF : C0, :] = msg[at + DS : at + DS + DF, :]
        w[r, C0 - DF : C0, :] = weight(msg[at + DS + DF : at + DEPTH, :])

    def put_right(r, msg, at):
        u[r, C1 : C1 + DS, :] = msg[at : at + DS, :]
        f[r, C1 : C1 + DF, :] = msg[at + DS : at + DS + DF, :]
        w[r, C1 : C1 + DF, :] = weight(msg[at + DS + DF : at + DEPTH, :])

    def lanes(left, right):
        def group(g, carry):
            base = pl.multiple_of(g * (8 * DEPTH), 8)
            for r in range(8):
                row, at = R0 + g * 8 + r, base + r * DEPTH
                u[row, C0 - DS : C0, :] = left[pl.ds(at, DS), :]
                f[row, C0 - DF : C0, :] = left[pl.ds(at + DS, DF), :]
                w[row, C0 - DF : C0, :] = weight(left[pl.ds(at + DS + DF, DF), :])
                u[row, C1 : C1 + DS, :] = right[pl.ds(at, DS), :]
                f[row, C1 : C1 + DF, :] = right[pl.ds(at + DS, DF), :]
                w[row, C1 : C1 + DF, :] = weight(right[pl.ds(at + DS + DF, DF), :])
            return carry

        lax.fori_loop(0, N // 8, group, 0)

    lane_even = parity("lane")

    @pl.when(lane_even)
    def _():
        lanes(ro, re)

    @pl.when(jnp.logical_not(lane_even))
    def _():
        lanes(re, ro)

    def bands(above, below, above_c, below_c):
        own = slice(C0, C1)
        for k in range(DS):
            u[k, own, :] = above[k]
            u[R1 + k, own, :] = below[k]
        for k in range(DF):
            f[R0 - DF + k, own, :] = above[DS + k]
            w[R0 - DF + k, own, :] = weight(above[DS + DF + k])
            f[R1 + k, own, :] = below[DS + k]
            w[R1 + k, own, :] = weight(below[DS + DF + k])
            for msg, row in ((above_c, R0 - DF + k), (below_c, R1 + k)):
                put_left(row, msg, k * DEPTH)
                put_right(row, msg, (DF + k) * DEPTH)

    band_even = parity("band")

    @pl.when(band_even)
    def _():
        bands(bo, be, co, ce)

    @pl.when(jnp.logical_not(band_even))
    def _():
        bands(be, bo, ce, co)

    sweep_rows(u, v, w, f, 1, ROWS - 1, FINE_SEGMENTS)
    sweep_rows(v, u, w, f, 2, ROWS - 2, FINE_SEGMENTS)
    sweep_rows(u, v, w, f, 3, ROWS - 3, FINE_SEGMENTS)

    def block(i, carry):
        total = jnp.zeros((N, L), f32)
        for k in range(RATIO):
            q = i * RATIO + k
            r = R0 + q
            total = total + (
                f[r, C0:C1, :]
                + (v[r - 1, C0:C1, :] + v[r + 1, C0:C1, :])
                + (v[r, C0 - 1 : C1 - 1, :] + v[r, C0 + 1 : C1 + 1, :])
                - a4[q] * v[r, C0:C1, :]
            )
        cl[i] = gather_columns(line, total)
        return carry

    lax.fori_loop(0, C, block, 0)
    pack_coarse_lanes(lambda i: cl[i], l_even, l_odd)
    for i in range(C):
        mext[H + i, CC0 : CC0 + C, :] = cm[i]
    place_coarse_lanes(mext, mre, mro)
    pack_coarse_bands(mext, mb_even, mb_odd)


def coarse_bands(cl, re, ro, lext, b_even, b_odd):
    for i in range(C):
        lext[H + i, CC0 : CC0 + C, :] = cl[i]
    place_coarse_lanes(lext, re, ro)
    pack_coarse_bands(lext, b_even, b_odd)


def after(v, f, w, mext_in, lext_in, mbe, mbo, lbe, lbo, out, mext, lext, a, b, wide, t, s):
    span = slice(CC0 - H, CC0 + C + H)
    for i in range(C):
        mext[H + i, span, :] = mext_in[H + i, span, :]
        lext[H + i, span, :] = lext_in[H + i, span, :]
    place_coarse_bands(mext, mbe, mbo)
    place_coarse_bands(lext, lbe, lbo)

    def first(r, carry):
        wc = weight(mext[r, 0:CCOLS, :])
        mext[r, 0:CCOLS, :] = wc
        a[r, 0:CCOLS, :] = wc * lext[r, 0:CCOLS, :]
        return carry

    lax.fori_loop(0, CR, first, 0)
    src, dst = a, b
    for k in range(1, INNER):
        if k <= 4:
            segments = ((4, 8), (8, 40), (40, 44))
        elif k <= 12:
            segments = ((8, 40),)
        sweep_rows(src, dst, mext, lext, k, CR - k, segments)
        src, dst = dst, src
    for i in range(-1, C + 1):
        row = src[H + i, CC0 - 1 : CC0 + C + 1, :]
        for k in range(RATIO):
            wide[pl.ds(k, C + 2, stride=RATIO), :] = row
        for k in range(RATIO):
            q = i * RATIO + k
            if -AFTER <= q < N + AFTER:
                r = R0 + q
                t[r, C0 - 4 : C0 + N + 4, :] = v[r, C0 - 4 : C0 + N + 4, :] + wide[...]
    sweep_rows(t, s, w, f, R0 - 1, R0 + N + 1, ((C0 - 4, C0), (C0, C0 + N), (C0 + N, C0 + N + 4)))

    def last(g, carry):
        for k in range(2):
            q = 2 * g + k
            r = R0 + q
            C1 = C0 + N
            around = (
                (s[r - 1, C0:C1, :] + s[r + 1, C0:C1, :])
                + (s[r, C0 - 1 : C1 - 1, :] + s[r, C0 + 1 : C1 + 1, :])
                + f[r, C0:C1, :]
            )
            out[q] = 0.2 * s[r, C0:C1, :] + w[r, C0:C1, :] * around
        return carry

    lax.fori_loop(0, N // 2, last, 0)


def swap_even(x, axis):
    n = lax.axis_size(axis)
    return lax.ppermute(x, axis, [(i, i ^ 1) for i in range(n)])


def swap_odd(x, axis):
    n = lax.axis_size(axis)
    return lax.ppermute(x, axis, [(i, (i + 1) % n if i % 2 else (i - 1) % n) for i in range(n)])


def shards(load, start, mass):
    dma = pltpu.SemaphoreType.DMA
    lane_msg, band_msg = sds(N * DEPTH, L), sds(DEPTH, N, L)
    me, mo, be, bo = call(
        pack_fine,
        [lane_msg, lane_msg, band_msg, band_msg],
        [ANY] * 3,
        [pltpu.VMEM((3, 2, N, 8, L), f32), dma((3, 2)), dma((2, 3))],
        name="pack_fine",
    )(load, start, mass)
    ro, re = swap_odd(mo, "lane"), swap_even(me, "lane")
    rbo, rbe = swap_odd(bo, "band"), swap_even(be, "band")

    fine = sds(ROWS, COLS, L)
    lane_coarse, band_coarse = sds(C * H, L), sds(BANDMSG, L)
    u, f, w, a4, cm, mme, mmo = call(
        prepare,
        [fine, fine, fine, sds(N, N, L), sds(C, C, L), lane_coarse, lane_coarse],
        [ANY] * 3,
        [pltpu.VMEM((N, L), f32), dma((3,))],
        flops=10**8,
        name="prepare",
    )(load, start, mass)
    rmo, rme = swap_odd(mmo, "lane"), swap_even(mme, "lane")

    corner = sds(2 * DF * DEPTH, L)
    ce, co = call(pack_corners, [corner, corner], [VM] * 2, name="pack_corners")(re, ro)
    rco, rce = swap_odd(co, "band"), swap_even(ce, "band")

    coarse = sds(CR, CCOLS, L)
    v, f, w, mext, le, lo, mbe, mbo, cl = call(
        before,
        [fine, fine, fine, coarse, lane_coarse, lane_coarse, band_coarse, band_coarse, sds(C, C, L)],
        [VM] * 13,
        [pltpu.VMEM((ROWS, COLS, L), f32), pltpu.VMEM((N, L), f32)],
        aliases={1: 1, 2: 2},
        flops=10**8,
        name="before",
    )(u, f, w, a4, cm, re, ro, rbe, rbo, rce, rco, rme, rmo)
    rlo, rle = swap_odd(lo, "lane"), swap_even(le, "lane")
    rmbo, rmbe = swap_odd(mbo, "band"), swap_even(mbe, "band")

    lext, lbe, lbo = call(
        coarse_bands, [coarse, band_coarse, band_coarse], [VM] * 3, name="coarse_bands"
    )(cl, rle, rlo)
    rlbo, rlbe = swap_odd(lbo, "band"), swap_even(lbe, "band")

    coarse_buf = pltpu.VMEM((CR, CCOLS, L), f32)
    fine_buf = pltpu.VMEM((ROWS, COLS, L), f32)
    (out,) = call(
        after,
        [sds(N, N, L)],
        [VM] * 9,
        [coarse_buf] * 4 + [pltpu.VMEM((N + 8, L), f32), fine_buf, fine_buf],
        flops=10**8,
        name="after",
        inner=False,
    )(v, f, w, mext, lext, rmbe, rmbo, rlbe, rlbo)
    return out


def solution(mesh):
    spec = P("band", "lane", None)
    return jax.shard_map(
        shards, mesh=mesh, in_specs=(spec, spec, spec), out_specs=spec, check_vma=False
    )
```

profile of v0, /device:TPU:1, one launch (start us, length us, event | category | flops | bytes accessed | tf_op | source)
XLA Modules:
  0.0 90.3 jit_solution(14269748562341323144)
XLA Ops:
  0.0 0.0 copy-start
  0.0 1.6 %copy-done = f32[64,64,128]{2,1,0:T(8,128)S(1)} copy-done((f32[64,64,128]{2,1,0:T(8,128)S(1)}, f32[64,64,128]{2,1,0:T(8,128)}, u32[]{:S(2)}) %copy-start) | copy-done | bytes 2097176
  1.6 0.0 copy-start.1
  1.6 1.6 %copy-done.1 = f32[64,64,128]{2,1,0:T(8,128)S(1)} copy-done((f32[64,64,128]{2,1,0:T(8,128)S(1)}, f32[64,64,128]{2,1,0:T(8,128)}, u32[]{:S(2)}) %copy-start.1) | copy-done | bytes 2097176
  3.2 0.0 copy-start.2
  3.2 1.6 %copy-done.2 = f32[64,64,128]{2,1,0:T(8,128)S(1)} copy-done((f32[64,64,128]{2,1,0:T(8,128)S(1)}, f32[64,64,128]{2,1,0:T(8,128)}, u32[]{:S(2)}) %copy-start.2) | copy-done | bytes 2097176
  4.8 1.6 %pack_fine.1 = (f32[832,128]{1,0:T(8,128)S(1)}, f32[832,128]{1,0:T(8,128)S(1)}, f32[13,64,128]{2,1,0:T(8,128)S(1)}, f32[13,64,128]{2,1,0:T(8,128)S(1)}) custom-call(f32[64,64,128]{2,1,0:T(8,128)S(1)} %copy-done, f32[64,64,128]{2,1,0:T(8,128)S(1)} %copy-done.1, f32[64,64,128]{2,1,0:T(8,128)S(1)} %copy-done.2), custom_call_target="tpu_custom_call" | custom-call | flops 1000000 | bytes 8000000 | tf_op jit(solution)/shard_map/pack_fine/pallas_call | solution.py:453
  6.4 2.1 %collective-permute-start = (f32[832,128]{1,0:T(8,128)S(1)}, f32[832,128]{1,0:T(8,128)S(1)}, u32[]{:S(2)}, u32[]{:S(2)}) collective-permute-start(f32[832,128]{1,0:T(8,128)S(1)} %get-tuple-element.35), channel_id=1, source_target_pairs={{0,1},{1,0},{2,3},{3,2},{4,5},{5,4},{6,7},{7,6},{8,9},{9,8},{10,11... | collective-permute-start | bytes 1277960 | tf_op jit(solution)/shard_map/ppermute | solution.py:442
  8.6 10.9 %collective-permute-start.1 = (f32[832,128]{1,0:T(8,128)S(1)}, f32[832,128]{1,0:T(8,128)S(1)}, u32[]{:S(2)}, u32[]{:S(2)}) collective-permute-start(f32[832,128]{1,0:T(8,128)S(1)} %get-tuple-element.36), channel_id=1, source_target_pairs={{0,31},{1,2},{2,1},{3,4},{4,3},{5,6},{6,5},{7,8},{8,7},{9,10},{10,... | collective-permute-start | bytes 1277960 | tf_op jit(solution)/shard_map/ppermute | solution.py:447
  19.4 1.2 %collective-permute-start.2 = (f32[13,64,128]{2,1,0:T(8,128)S(1)}, f32[13,64,128]{2,1,0:T(8,128)S(1)}, u32[]{:S(2)}, u32[]{:S(2)}) collective-permute-start(f32[13,64,128]{2,1,0:T(8,128)S(1)} %get-tuple-element.37), channel_id=1, source_target_pairs={{0,32},{32,0},{64,96},{96,64},{128,160},{160,128},{192,224},{224,1... | collective-permute-start | bytes 1277960 | tf_op jit(solution)/shard_map/ppermute | solution.py:442
  20.7 0.6 collective-permute-start.3
  21.3 1.2 %prepare.1 = (f32[74,80,128]{2,1,0:T(8,128)S(1)}, f32[74,80,128]{2,1,0:T(8,128)S(1)}, f32[74,80,128]{2,1,0:T(8,128)S(1)}, f32[64,64,128]{2,1,0:T(8,128)S(1)}, f3...) custom-call(f32[64,64,128]{2,1,0:T(8,128)S(1)} %copy-done, f32[64,64,128]{2,1,0:T(8,128)S(1)} %copy-done.1, ...), custom_call_target="tpu_custom_call" | custom-call | flops 100000000 | bytes 8000000 | tf_op jit(solution)/shard_map/prepare/pallas_call | solution.py:465
  22.5 0.1 collective-permute-start.6
  22.6 0.0 collective-permute-done.m_even.re
  22.6 7.0 %collective-permute-start.7 = (f32[208,128]{1,0:T(8,128)S(1)}, f32[208,128]{1,0:T(8,128)S(1)}, u32[]{:S(2)}, u32[]{:S(2)}) collective-permute-start(f32[208,128]{1,0:T(8,128)S(1)} %get-tuple-element.42), channel_id=1, source_target_pairs={{0,31},{1,2},{2,1},{3,4},{4,3},{5,6},{6,5},{7,8},{8,7},{9,10},{10,... | collective-permute-start | bytes 319496 | tf_op jit(solution)/shard_map/ppermute | solution.py:447
  29.6 5.7 %collective-permute-done.1.m_odd.ro = f32[832,128]{1,0:T(8,128)S(1)} collective-permute-done((f32[832,128]{1,0:T(8,128)S(1)}, f32[832,128]{1,0:T(8,128)S(1)}, u32[]{:S(2)}, u32[]{:S(2)}) %collective-permute-start.1) | collective-permute-done | bytes 426016 | tf_op jit(solution)/shard_map/ppermute | solution.py:447
  35.3 5.2 %collective-permute-start.4 = (f32[104,128]{1,0:T(8,128)S(1)}, f32[104,128]{1,0:T(8,128)S(1)}, u32[]{:S(2)}, u32[]{:S(2)}) collective-permute-start(f32[104,128]{1,0:T(8,128)S(1)} %get-tuple-element.39), channel_id=1, source_target_pairs={{0,32},{32,0},{64,96},{96,64},{128,160},{160,128},{192,224},{224,1... | collective-permute-start | bytes 159752 | tf_op jit(solution)/shard_map/ppermute | solution.py:442
  40.6 0.0 collective-permute-done.6.mre
  40.6 1.5 %collective-permute-start.5 = (f32[104,128]{1,0:T(8,128)S(1)}, f32[104,128]{1,0:T(8,128)S(1)}, u32[]{:S(2)}, u32[]{:S(2)}) collective-permute-start(f32[104,128]{1,0:T(8,128)S(1)} %get-tuple-element.40), channel_id=1, source_target_pairs={{0,224},{32,64},{64,32},{96,128},{128,96},{160,192},{192,160},{224... | collective-permute-start | bytes 159752 | tf_op jit(solution)/shard_map/ppermute | solution.py:447
  42.1 9.0 %collective-permute-done.7.mro = f32[208,128]{1,0:T(8,128)S(1)} collective-permute-done((f32[208,128]{1,0:T(8,128)S(1)}, f32[208,128]{1,0:T(8,128)S(1)}, u32[]{:S(2)}, u32[]{:S(2)}) %collective-permute-start.7) | collective-permute-done | bytes 106528 | tf_op jit(solution)/shard_map/ppermute | solution.py:447
  51.1 0.0 collective-permute-done.2.be
  51.1 0.0 collective-permute-done.3.bo
  51.1 0.0 collective-permute-done.4.ce
  51.1 3.1 %collective-permute-done.5.co = f32[104,128]{1,0:T(8,128)S(1)} collective-permute-done((f32[104,128]{1,0:T(8,128)S(1)}, f32[104,128]{1,0:T(8,128)S(1)}, u32[]{:S(2)}, u32[]{:S(2)}) %collective-permute-start.5) | collective-permute-done | bytes 53280 | tf_op jit(solution)/shard_map/ppermute | solution.py:447
  54.3 5.0 %before.1 = (f32[74,80,128]{2,1,0:T(8,128)S(1)}, f32[74,80,128]{2,1,0:T(8,128)S(1)}, f32[74,80,128]{2,1,0:T(8,128)S(1)}, f32[42,48,128]{2,1,0:T(8,128)S(1)}, f32...) custom-call(f32[74,80,128]{2,1,0:T(8,128)S(1)} %get-tuple-element.30, ...), custom_call_target="tpu_custom_call", output_to_operand_aliasing={{1}: (1, {}), {2}: (2, {})} | custom-call | flops 100000000 | bytes 8000000 | tf_op jit(solution)/shard_map/before/pallas_call | solution.py:480
  59.2 0.1 collective-permute-start.8
  59.3 7.0 %collective-permute-start.9 = (f32[208,128]{1,0:T(8,128)S(1)}, f32[208,128]{1,0:T(8,128)S(1)}, u32[]{:S(2)}, u32[]{:S(2)}) collective-permute-start(f32[208,128]{1,0:T(8,128)S(1)} %get-tuple-element.49), channel_id=1, source_target_pairs={{0,31},{1,2},{2,1},{3,4},{4,3},{5,6},{6,5},{7,8},{8,7},{9,10},{10,... | collective-permute-start | bytes 319496 | tf_op jit(solution)/shard_map/ppermute | solution.py:447
  66.4 2.9 %collective-permute-start.10 = (f32[392,128]{1,0:T(8,128)S(1)}, f32[392,128]{1,0:T(8,128)S(1)}, u32[]{:S(2)}, u32[]{:S(2)}) collective-permute-start(f32[392,128]{1,0:T(8,128)S(1)} %get-tuple-element.51), channel_id=1, source_target_pairs={{0,32},{32,0},{64,96},{96,64},{128,160},{160,128},{192,224},{224,1... | collective-permute-start | bytes 602120 | tf_op jit(solution)/shard_map/ppermute | solution.py:442
  69.3 0.1 collective-permute-start.11
  69.4 0.0 collective-permute-done.8.re
  69.4 4.8 %collective-permute-done.9.ro = f32[208,128]{1,0:T(8,128)S(1)} collective-permute-done((f32[208,128]{1,0:T(8,128)S(1)}, f32[208,128]{1,0:T(8,128)S(1)}, u32[]{:S(2)}, u32[]{:S(2)}) %collective-permute-start.9) | collective-permute-done | bytes 106528 | tf_op jit(solution)/shard_map/ppermute | solution.py:447
  74.1 0.1 coarse_bands.1
  74.2 0.9 %collective-permute-start.12 = (f32[392,128]{1,0:T(8,128)S(1)}, f32[392,128]{1,0:T(8,128)S(1)}, u32[]{:S(2)}, u32[]{:S(2)}) collective-permute-start(f32[392,128]{1,0:T(8,128)S(1)} %get-tuple-element.53), channel_id=1, source_target_pairs={{0,32},{32,0},{64,96},{96,64},{128,160},{160,128},{192,224},{224,1... | collective-permute-start | bytes 602120 | tf_op jit(solution)/shard_map/ppermute | solution.py:442
  75.1 0.0 collective-permute-start.13
  75.1 0.0 collective-permute-done.10.mbe
  75.1 1.5 %collective-permute-done.11.mbo = f32[392,128]{1,0:T(8,128)S(1)} collective-permute-done((f32[392,128]{1,0:T(8,128)S(1)}, f32[392,128]{1,0:T(8,128)S(1)}, u32[]{:S(2)}, u32[]{:S(2)}) %collective-permute-start.11) | collective-permute-done | bytes 200736 | tf_op jit(solution)/shard_map/ppermute | solution.py:447
  76.6 0.0 collective-permute-done.12.lbe
  76.6 6.0 %collective-permute-done.13.lbo = f32[392,128]{1,0:T(8,128)S(1)} collective-permute-done((f32[392,128]{1,0:T(8,128)S(1)}, f32[392,128]{1,0:T(8,128)S(1)}, u32[]{:S(2)}, u32[]{:S(2)}) %collective-permute-start.13) | collective-permute-done | bytes 200736 | tf_op jit(solution)/shard_map/ppermute | solution.py:447
  82.6 7.6 %after.1 = f32[64,64,128]{2,1,0:T(8,128)} custom-call(f32[74,80,128]{2,1,0:T(8,128)S(1)} %get-tuple-element.43.v, f32[74,80,128]{2,1,0:T(8,128)S(1)} %get-tuple-element.44.f, f32[74,80,128]{2,1,0:T(8,128)S(1)} %get-tuple-element.45.w, f32[42,48,128]{2,1,0:T(8,128)S(1)} %get-tuple-element.46.mext_in, f32[42,48,128]{2,1,0:T(8,128)S(1)} %get-tuple-element.50.lext_in, ...), custom_call_target="tpu_custom_call" | custom-call | flops 100000000 | bytes 8000000 | tf_op jit(solution)/shard_map/after/pallas_call | solution.py:499
  (1 shorter events, 0.0 us)
Async XLA Ops:
  0.0 1.6 %copy-start = (f32[64,64,128]{2,1,0:T(8,128)S(1)}, f32[64,64,128]{2,1,0:T(8,128)}, u32[]{:S(2)}) copy-start(f32[64,64,128]{2,1,0:T(8,128)} %load.3) | copy-start | bytes 6291460
  1.6 1.6 %copy-start.1 = (f32[64,64,128]{2,1,0:T(8,128)S(1)}, f32[64,64,128]{2,1,0:T(8,128)}, u32[]{:S(2)}) copy-start(f32[64,64,128]{2,1,0:T(8,128)} %start.3) | copy-start | bytes 6291460
  3.2 1.6 %copy-start.2 = (f32[64,64,128]{2,1,0:T(8,128)S(1)}, f32[64,64,128]{2,1,0:T(8,128)}, u32[]{:S(2)}) copy-start(f32[64,64,128]{2,1,0:T(8,128)} %mass.3) | copy-start | bytes 6291460
  6.4 16.2 %collective-permute-start = (f32[832,128]{1,0:T(8,128)S(1)}, f32[832,128]{1,0:T(8,128)S(1)}, u32[]{:S(2)}, u32[]{:S(2)}) collective-permute-start(f32[832,128]{1,0:T(8,128)S(1)} %get-tuple-element.35), channel_id=1, source_target_pairs={{0,1},{1,0},{2,3},{3,2},{4,5},{5,4},{6,7},{7,6},{8,9},{9,8},{10,11... | collective-permute-start | bytes 1277960 | tf_op jit(solution)/shard_map/ppermute | solution.py:442
  8.6 26.8 %collective-permute-start.1 = (f32[832,128]{1,0:T(8,128)S(1)}, f32[832,128]{1,0:T(8,128)S(1)}, u32[]{:S(2)}, u32[]{:S(2)}) collective-permute-start(f32[832,128]{1,0:T(8,128)S(1)} %get-tuple-element.36), channel_id=1, source_target_pairs={{0,31},{1,2},{2,1},{3,4},{4,3},{5,6},{6,5},{7,8},{8,7},{9,10},{10,... | collective-permute-start | bytes 1277960 | tf_op jit(solution)/shard_map/ppermute | solution.py:447
  19.4 31.7 %collective-permute-start.2 = (f32[13,64,128]{2,1,0:T(8,128)S(1)}, f32[13,64,128]{2,1,0:T(8,128)S(1)}, u32[]{:S(2)}, u32[]{:S(2)}) collective-permute-start(f32[13,64,128]{2,1,0:T(8,128)S(1)} %get-tuple-element.37), channel_id=1, source_target_pairs={{0,32},{32,0},{64,96},{96,64},{128,160},{160,128},{192,224},{224,1... | collective-permute-start | bytes 1277960 | tf_op jit(solution)/shard_map/ppermute | solution.py:442
  20.7 30.4 %collective-permute-start.3 = (f32[13,64,128]{2,1,0:T(8,128)S(1)}, f32[13,64,128]{2,1,0:T(8,128)S(1)}, u32[]{:S(2)}, u32[]{:S(2)}) collective-permute-start(f32[13,64,128]{2,1,0:T(8,128)S(1)} %get-tuple-element.38), channel_id=1, source_target_pairs={{0,224},{32,64},{64,32},{96,128},{128,96},{160,192},{192,160},{224... | collective-permute-start | bytes 1277960 | tf_op jit(solution)/shard_map/ppermute | solution.py:447
  22.5 18.1 %collective-permute-start.6 = (f32[208,128]{1,0:T(8,128)S(1)}, f32[208,128]{1,0:T(8,128)S(1)}, u32[]{:S(2)}, u32[]{:S(2)}) collective-permute-start(f32[208,128]{1,0:T(8,128)S(1)} %get-tuple-element.41), channel_id=1, source_target_pairs={{0,1},{1,0},{2,3},{3,2},{4,5},{5,4},{6,7},{7,6},{8,9},{9,8},{10,11... | collective-permute-start | bytes 319496 | tf_op jit(solution)/shard_map/ppermute | solution.py:442
  22.6 28.5 %collective-permute-start.7 = (f32[208,128]{1,0:T(8,128)S(1)}, f32[208,128]{1,0:T(8,128)S(1)}, u32[]{:S(2)}, u32[]{:S(2)}) collective-permute-start(f32[208,128]{1,0:T(8,128)S(1)} %get-tuple-element.42), channel_id=1, source_target_pairs={{0,31},{1,2},{2,1},{3,4},{4,3},{5,6},{6,5},{7,8},{8,7},{9,10},{10,... | collective-permute-start | bytes 319496 | tf_op jit(solution)/shard_map/ppermute | solution.py:447
  35.3 15.8 %collective-permute-start.4 = (f32[104,128]{1,0:T(8,128)S(1)}, f32[104,128]{1,0:T(8,128)S(1)}, u32[]{:S(2)}, u32[]{:S(2)}) collective-permute-start(f32[104,128]{1,0:T(8,128)S(1)} %get-tuple-element.39), channel_id=1, source_target_pairs={{0,32},{32,0},{64,96},{96,64},{128,160},{160,128},{192,224},{224,1... | collective-permute-start | bytes 159752 | tf_op jit(solution)/shard_map/ppermute | solution.py:442
  40.6 13.7 %collective-permute-start.5 = (f32[104,128]{1,0:T(8,128)S(1)}, f32[104,128]{1,0:T(8,128)S(1)}, u32[]{:S(2)}, u32[]{:S(2)}) collective-permute-start(f32[104,128]{1,0:T(8,128)S(1)} %get-tuple-element.40), channel_id=1, source_target_pairs={{0,224},{32,64},{64,32},{96,128},{128,96},{160,192},{192,160},{224... | collective-permute-start | bytes 159752 | tf_op jit(solution)/shard_map/ppermute | solution.py:447
  59.2 10.1 %collective-permute-start.8 = (f32[208,128]{1,0:T(8,128)S(1)}, f32[208,128]{1,0:T(8,128)S(1)}, u32[]{:S(2)}, u32[]{:S(2)}) collective-permute-start(f32[208,128]{1,0:T(8,128)S(1)} %get-tuple-element.48), channel_id=1, source_target_pairs={{0,1},{1,0},{2,3},{3,2},{4,5},{5,4},{6,7},{7,6},{8,9},{9,8},{10,11... | collective-permute-start | bytes 319496 | tf_op jit(solution)/shard_map/ppermute | solution.py:442
  59.3 14.8 %collective-permute-start.9 = (f32[208,128]{1,0:T(8,128)S(1)}, f32[208,128]{1,0:T(8,128)S(1)}, u32[]{:S(2)}, u32[]{:S(2)}) collective-permute-start(f32[208,128]{1,0:T(8,128)S(1)} %get-tuple-element.49), channel_id=1, source_target_pairs={{0,31},{1,2},{2,1},{3,4},{4,3},{5,6},{6,5},{7,8},{8,7},{9,10},{10,... | collective-permute-start | bytes 319496 | tf_op jit(solution)/shard_map/ppermute | solution.py:447
  66.4 8.7 %collective-permute-start.10 = (f32[392,128]{1,0:T(8,128)S(1)}, f32[392,128]{1,0:T(8,128)S(1)}, u32[]{:S(2)}, u32[]{:S(2)}) collective-permute-start(f32[392,128]{1,0:T(8,128)S(1)} %get-tuple-element.51), channel_id=1, source_target_pairs={{0,32},{32,0},{64,96},{96,64},{128,160},{160,128},{192,224},{224,1... | collective-permute-start | bytes 602120 | tf_op jit(solution)/shard_map/ppermute | solution.py:442
  69.3 7.3 %collective-permute-start.11 = (f32[392,128]{1,0:T(8,128)S(1)}, f32[392,128]{1,0:T(8,128)S(1)}, u32[]{:S(2)}, u32[]{:S(2)}) collective-permute-start(f32[392,128]{1,0:T(8,128)S(1)} %get-tuple-element.52), channel_id=1, source_target_pairs={{0,224},{32,64},{64,32},{96,128},{128,96},{160,192},{192,160},{224... | collective-permute-start | bytes 602120 | tf_op jit(solution)/shard_map/ppermute | solution.py:447
  74.2 2.4 %collective-permute-start.12 = (f32[392,128]{1,0:T(8,128)S(1)}, f32[392,128]{1,0:T(8,128)S(1)}, u32[]{:S(2)}, u32[]{:S(2)}) collective-permute-start(f32[392,128]{1,0:T(8,128)S(1)} %get-tuple-element.53), channel_id=1, source_target_pairs={{0,32},{32,0},{64,96},{96,64},{128,160},{160,128},{192,224},{224,1... | collective-permute-start | bytes 602120 | tf_op jit(solution)/shard_map/ppermute | solution.py:442
  75.1 7.5 %collective-permute-start.13 = (f32[392,128]{1,0:T(8,128)S(1)}, f32[392,128]{1,0:T(8,128)S(1)}, u32[]{:S(2)}, u32[]{:S(2)}) collective-permute-start(f32[392,128]{1,0:T(8,128)S(1)} %get-tuple-element.54), channel_id=1, source_target_pairs={{0,224},{32,64},{64,32},{96,128},{128,96},{160,192},{192,160},{224... | collective-permute-start | bytes 602120 | tf_op jit(solution)/shard_map/ppermute | solution.py:447
where the time goes:
time: 90.4 us; the launch traced here: 90.3 us
  starting transfers between devices  39.7 us (44%)
  waiting for transfers between devices  30.2 us (33%)
  Pallas kernels  15.5 us (17%)
  local copies, waits for them, and re-layouts  4.77 us (5%)
    ppermute x7, waiting for transfers between devices, swap_odd(): lax.ppermute(x, axis, [(i, (i + 1) % n if i % 2 else (i - 1) % n) for i i...  30.2 us
    ppermute x7, starting transfers between devices, swap_odd(): lax.ppermute(x, axis, [(i, (i + 1) % n if i % 2 else (i - 1) % n) for i i...  27.1 us
    ppermute x7, starting transfers between devices, swap_even(): return lax.ppermute(x, axis, [(i, i ^ 1) for i in range(n)])  12.6 us
    pallas_call x1, Pallas kernels, shards(): call(after, [sds(N, N, L)], [VM] * 9, [coarse_buf] * 4 + [pltpu.VMEM((N +...  7.64 us
    pallas_call x1, Pallas kernels, shards(): call(before, [fine, fine, fine, coarse, lane_coarse, lane_coarse, band_co...  4.97 us
    unnamed x6, local copies, waits for them, and re-layouts  4.77 us
  transfers between devices with their start and end apart: 14, of which 6 were waited for; matrix products, arithmetic and copies ran while one was open for 0% of the time, Pallas kernels for 1%

commit v1 on v0

--- a/solution.py
+++ b/solution.py
@@ -41,7 +41,7 @@
 
 
 VM = pl.BlockSpec(memory_space=pltpu.VMEM)
-ANY = pl.BlockSpec(memory_space=pl.ANY)
+HBM = pl.BlockSpec(memory_space=pltpu.HBM)
 
 
 def call(body, outs, ins, scratch=(), out_specs=None, aliases=None, flops=10**6, name=None, inner=True):
@@ -58,9 +58,10 @@
     )
 
 
-def pack_fine(load, start, mass, m_even, m_odd, b_even, b_odd, side, sem_side, sem_band):
+def pack_fine(load, start, mass_hbm, m_even, m_odd, b_even, b_odd, mass, cm, side, line, sem_side, sem_mass, sem_band):
+    whole = pltpu.make_async_copy(mass_hbm, mass, sem_mass.at[0])
     copies = []
-    for k, src in enumerate((start, load, mass)):
+    for k, src in enumerate((start, load)):
         for s, at in enumerate((0, N - 8)):
             copies.append(
                 pltpu.make_async_copy(src.at[:, pl.ds(at, 8)], side.at[k, s], sem_side.at[k, s])
@@ -69,7 +70,7 @@
     bands = []
     for which, (dst, bottom) in enumerate(((b_even, even), (b_odd, jnp.logical_not(even)))):
         at = 0
-        for k, (src, depth) in enumerate(((start, DS), (load, DF), (mass, DF))):
+        for k, (src, depth) in enumerate(((start, DS), (load, DF), (mass_hbm, DF))):
             first = jnp.where(bottom, N - depth, 0)
             bands.append(
                 pltpu.make_async_copy(
@@ -79,17 +80,19 @@
             at += depth
     for c in copies:
         c.start()
+    whole.start()
     for c in bands:
         c.start()
     for c in copies:
         c.wait()
+    lane_even = parity("lane")
 
     def pack(dst, s):
         def group(g, carry):
             base = pl.multiple_of(g * (8 * DEPTH), 8)
             for r in range(8):
                 at = r * DEPTH
-                for k, depth in enumerate((DS, DF, DF)):
+                for k, depth in enumerate((DS, DF)):
                     lo = 0 if s == 0 else 8 - depth
                     dst[pl.ds(base + at, depth), :] = side[k, s, g * 8 + r, lo : lo + depth, :]
                     at += depth
@@ -97,8 +100,6 @@
 
         lax.fori_loop(0, N // 8, group, 0)
 
-    lane_even = parity("lane")
-
     @pl.when(lane_even)
     def _():
         pack(m_even, 1)
@@ -108,6 +109,38 @@
     def _():
         pack(m_even, 0)
         pack(m_odd, 1)
+
+    whole.wait()
+
+    def pack_mass(right, left):
+        def group(g, carry):
+            base = pl.multiple_of(g * (8 * DEPTH), 8)
+            for half in range(2):
+                total = None
+                for k in range(RATIO):
+                    r = half * RATIO + k
+                    at = r * DEPTH + DS + DF
+                    row = mass[g * 8 + r]
+                    total = row if total is None else total + row
+                    right[pl.ds(base + at, DF), :] = row[N - DF :, :]
+                    left[pl.ds(base + at, DF), :] = row[:DF, :]
+                cm[2 * g + half] = gather_columns(line.at[half], total)
+            return carry
+
+        lax.fori_loop(0, N // 8, group, 0)
+        for i in range(C):
+            at = N * DEPTH + i * H
+            row = cm[i]
+            right[at : at + H, :] = row[C - H :, :]
+            left[at : at + H, :] = row[:H, :]
+
+    @pl.when(lane_even)
+    def _():
+        pack_mass(m_even, m_odd)
+
+    @pl.when(jnp.logical_not(lane_even))
+    def _():
+        pack_mass(m_odd, m_even)
 
     for c in bands:
         c.wait()
@@ -162,11 +195,12 @@
         put(m_odd, m_even)
 
 
-def place_coarse_lanes(ext, m_even, m_odd):
+def place_coarse_lanes(ext, m_even, m_odd, at=0):
     def put(left, right):
         for i in range(C):
-            ext[H + i, CC0 - H : CC0, :] = left[i * H : (i + 1) * H, :]
-            ext[H + i, CC0 + C : CC0 + C + H, :] = right[i * H : (i + 1) * H, :]
+            lo = at + i * H
+            ext[H + i, CC0 - H : CC0, :] = left[lo : lo + H, :]
+            ext[H + i, CC0 + C : CC0 + C + H, :] = right[lo : lo + H, :]
 
     even = parity("lane")
 
@@ -253,39 +287,32 @@
     return total * (1.0 / RATIO)
 
 
-def prepare(load, start, mass, u, f, w, a4, cm, m_even, m_odd, line, sems):
+def prepare(load, start, mass, u, f, w, a4, sems):
     own = (pl.ds(R0, N), pl.ds(C0, N))
     copies = [
-        pltpu.make_async_copy(mass, a4, sems.at[0]),
-        pltpu.make_async_copy(load, f.at[own], sems.at[1]),
-        pltpu.make_async_copy(start, u.at[own], sems.at[2]),
+        pltpu.make_async_copy(load, f.at[own], sems.at[0]),
+        pltpu.make_async_copy(start, u.at[own], sems.at[1]),
     ]
     for c in copies:
         c.start()
-    copies[0].wait()
-
-    def block(i, carry):
-        total = jnp.zeros((N, L), f32)
-        for k in range(RATIO):
-            r = i * RATIO + k
-            m = a4[r]
-            total = total + m
-            a = 4.0 + m
+
+    def group(g, carry):
+        for k in range(2):
+            r = g * 2 + k
+            a = 4.0 + mass[r]
             a4[r] = a
             w[R0 + r, C0 : C0 + N, :] = 0.8 / a
-        cm[i] = gather_columns(line, total)
-        return carry
-
-    lax.fori_loop(0, C, block, 0)
-    pack_coarse_lanes(lambda i: cm[i], m_even, m_odd)
-    for c in copies[1:]:
+        return carry
+
+    lax.fori_loop(0, N // 2, group, 0)
+    for c in copies:
         c.wait()
 
 
 FINE_SEGMENTS = ((C0 - DF, C0), (C0, C0 + N), (C0 + N, C0 + N + DF))
 
 
-def before(u_in, f_in, w_in, a4, cm, re, ro, be, bo, ce, co, mre, mro, v, f, w, mext, l_even, l_odd, mb_even, mb_odd, cl, u, line):
+def before(u_in, f_in, w_in, a4, cm, re, ro, be, bo, ce, co, v, f, w, mext, l_even, l_odd, mb_even, mb_odd, cl, u, line):
     def rows_copy(g, carry):
         for k in range(2):
             r = R0 + 2 * g + k
@@ -376,7 +403,7 @@
     pack_coarse_lanes(lambda i: cl[i], l_even, l_odd)
     for i in range(C):
         mext[H + i, CC0 : CC0 + C, :] = cm[i]
-    place_coarse_lanes(mext, mre, mro)
+    place_coarse_lanes(mext, re, ro, N * DEPTH)
     pack_coarse_bands(mext, mb_even, mb_odd)
 
 
@@ -387,18 +414,29 @@
     pack_coarse_bands(lext, b_even, b_odd)
 
 
-def after(v, f, w, mext_in, lext_in, mbe, mbo, lbe, lbo, out, mext, lext, a, b, wide, t, s):
+def coarse_weights(mext, mbe, mbo, wext, ext):
     span = slice(CC0 - H, CC0 + C + H)
     for i in range(C):
-        mext[H + i, span, :] = mext_in[H + i, span, :]
+        ext[H + i, span, :] = mext[H + i, span, :]
+    place_coarse_bands(ext, mbe, mbo)
+
+    def group(g, carry):
+        for k in range(2):
+            r = g * 2 + k
+            wext[r] = weight(ext[r])
+        return carry
+
+    lax.fori_loop(0, CR // 2, group, 0)
+
+
+def after(v, f, w, mext, lext_in, lbe, lbo, out, lext, a, b, wide, t, s):
+    span = slice(CC0 - H, CC0 + C + H)
+    for i in range(C):
         lext[H + i, span, :] = lext_in[H + i, span, :]
-    place_coarse_bands(mext, mbe, mbo)
     place_coarse_bands(lext, lbe, lbo)
 
     def first(r, carry):
-        wc = weight(mext[r, 0:CCOLS, :])
-        mext[r, 0:CCOLS, :] = wc
-        a[r, 0:CCOLS, :] = wc * lext[r, 0:CCOLS, :]
+        a[r] = mext[r] * lext[r]
         return carry
 
     lax.fori_loop(0, CR, first, 0)
@@ -448,44 +486,45 @@
 
 
 def shards(load, start, mass):
+    load, start, mass = (pltpu.with_memory_space_constraint(x, pltpu.HBM) for x in (load, start, mass))
     dma = pltpu.SemaphoreType.DMA
-    lane_msg, band_msg = sds(N * DEPTH, L), sds(DEPTH, N, L)
-    me, mo, be, bo = call(
+    own, fine, corner = sds(N, N, L), sds(ROWS, COLS, L), sds(2 * DF * DEPTH, L)
+    lane_msg, band_msg = sds(N * DEPTH + C * H, L), sds(DEPTH, N, L)
+    lane_coarse, band_coarse = sds(C * H, L), sds(BANDMSG, L)
+    coarse, own_coarse = sds(CR, CCOLS, L), sds(C, C, L)
+    coarse_buf, fine_buf = pltpu.VMEM((CR, CCOLS, L), f32), pltpu.VMEM((ROWS, COLS, L), f32)
+
+    me, mo, be, bo, mass_in, cm = call(
         pack_fine,
-        [lane_msg, lane_msg, band_msg, band_msg],
-        [ANY] * 3,
-        [pltpu.VMEM((3, 2, N, 8, L), f32), dma((3, 2)), dma((2, 3))],
+        [lane_msg, lane_msg, band_msg, band_msg, own, own_coarse],
+        [HBM] * 3,
+        [pltpu.VMEM((2, 2, N, 8, L), f32), pltpu.VMEM((2, N, L), f32), dma((2, 2)), dma((1,)), dma((2, 3))],
         name="pack_fine",
     )(load, start, mass)
     ro, re = swap_odd(mo, "lane"), swap_even(me, "lane")
     rbo, rbe = swap_odd(bo, "band"), swap_even(be, "band")
 
-    fine = sds(ROWS, COLS, L)
-    lane_coarse, band_coarse = sds(C * H, L), sds(BANDMSG, L)
-    u, f, w, a4, cm, mme, mmo = call(
+    u, f, w, a4 = call(
         prepare,
-        [fine, fine, fine, sds(N, N, L), sds(C, C, L), lane_coarse, lane_coarse],
-        [ANY] * 3,
-        [pltpu.VMEM((N, L), f32), dma((3,))],
+        [fine, fine, fine, own],
+        [HBM, HBM, VM],
+        [dma((2,))],
         flops=10**8,
         name="prepare",
-    )(load, start, mass)
-    rmo, rme = swap_odd(mmo, "lane"), swap_even(mme, "lane")
-
-    corner = sds(2 * DF * DEPTH, L)
+    )(load, start, mass_in)
+
     ce, co = call(pack_corners, [corner, corner], [VM] * 2, name="pack_corners")(re, ro)
     rco, rce = swap_odd(co, "band"), swap_even(ce, "band")
 
-    coarse = sds(CR, CCOLS, L)
     v, f, w, mext, le, lo, mbe, mbo, cl = call(
         before,
-        [fine, fine, fine, coarse, lane_coarse, lane_coarse, band_coarse, band_coarse, sds(C, C, L)],
-        [VM] * 13,
-        [pltpu.VMEM((ROWS, COLS, L), f32), pltpu.VMEM((N, L), f32)],
+        [fine, fine, fine, coarse, lane_coarse, lane_coarse, band_coarse, band_coarse, own_coarse],
+        [VM] * 11,
+        [fine_buf, pltpu.VMEM((N, L), f32)],
         aliases={1: 1, 2: 2},
         flops=10**8,
         name="before",
-    )(u, f, w, a4, cm, re, ro, rbe, rbo, rce, rco, rme, rmo)
+    )(u, f, w, a4, cm, re, ro, rbe, rbo, rce, rco)
     rlo, rle = swap_odd(lo, "lane"), swap_even(le, "lane")
     rmbo, rmbe = swap_odd(mbo, "band"), swap_even(mbe, "band")
 
@@ -493,18 +532,19 @@
         coarse_bands, [coarse, band_coarse, band_coarse], [VM] * 3, name="coarse_bands"
     )(cl, rle, rlo)
     rlbo, rlbe = swap_odd(lbo, "band"), swap_even(lbe, "band")
-
-    coarse_buf = pltpu.VMEM((CR, CCOLS, L), f32)
-    fine_buf = pltpu.VMEM((ROWS, COLS, L), f32)
+    (wext,) = call(
+        coarse_weights, [coarse], [VM] * 3, [coarse_buf], flops=10**7, name="coarse_weights"
+    )(mext, rmbe, rmbo)
+
     (out,) = call(
         after,
-        [sds(N, N, L)],
-        [VM] * 9,
-        [coarse_buf] * 4 + [pltpu.VMEM((N + 8, L), f32), fine_buf, fine_buf],
+        [own],
+        [VM] * 7,
+        [coarse_buf] * 3 + [pltpu.VMEM((N + 8, L), f32), fine_buf, fine_buf],
         flops=10**8,
         name="after",
         inner=False,
-    )(v, f, w, mext, lext, rmbe, rmbo, rlbe, rlbo)
+    )(v, f, w, wext, lext, rlbe, rlbo)
     return out
 
 

time: 90.4 us -> 86.2 us (0.954)
  starting transfers between devices: 39.7 us -> 27.5 us
  waiting for transfers between devices: 30.2 us -> 41 us
  local copies, waits for them, and re-layouts: 4.77 us -> 0 us
  Pallas kernels: 15.5 us -> 17.5 us
    ppermute x7 -> x6, starting transfers between devices: 27.1 us -> 16.7 us  [swap_odd(): lax.ppermute(x, axis, [(i, (i + 1) % n if i % 2 else (i - 1) % n) for i i...]
    ppermute x7 -> x6, waiting for transfers between devices: 30.2 us -> 40.4 us  [swap_odd(): lax.ppermute(x, axis, [(i, (i + 1) % n if i % 2 else (i - 1) % n) for i i...]
    unnamed x6 -> x0, local copies, waits for them, and re-layouts: 4.77 us -> none
    pallas_call x3 -> x4, Pallas kernels: 10.5 us -> 12.4 us  [the longest x1 7.27 us: shards(): call(after, [own], [VM] * 7, [coarse_buf] * 3 + [pltpu.VMEM((N + 8, L), f...]
    ppermute x7 -> x6, starting transfers between devices: 12.6 us -> 10.8 us  [swap_even(): return lax.ppermute(x, axis, [(i, i ^ 1) for i in range(n)])]
  transfers between devices with their start and end apart: 14 -> 12, of which waited for: 6 -> 6; matrix products, arithmetic and copies ran while one was open for 0% -> 0% of each run, Pallas kernels for 1% -> 3%
where the time goes in v1:
time: 86.2 us; the launch traced here: 86.1 us
  waiting for transfers between devices  41 us (48%)
  starting transfers between devices  27.5 us (32%)
  Pallas kernels  17.5 us (20%)
    ppermute x6, waiting for transfers between devices, swap_odd(): lax.ppermute(x, axis, [(i, (i + 1) % n if i % 2 else (i - 1) % n) for i i...  40.4 us
    ppermute x6, starting transfers between devices, swap_odd(): lax.ppermute(x, axis, [(i, (i + 1) % n if i % 2 else (i - 1) % n) for i i...  16.7 us
    ppermute x6, starting transfers between devices, swap_even(): return lax.ppermute(x, axis, [(i, i ^ 1) for i in range(n)])  10.8 us
    pallas_call x1, Pallas kernels, shards(): call(after, [own], [VM] * 7, [coarse_buf] * 3 + [pltpu.VMEM((N + 8, L), f...  7.27 us
    pallas_call x1, Pallas kernels, shards(): call(before, [fine, fine, fine, coarse, lane_coarse, lane_coarse, band_co...  4.97 us
    pallas_call x1, Pallas kernels, shards(): call(pack_fine, [lane_msg, lane_msg, band_msg, band_msg, own, own_coarse]...  2.51 us
    pallas_call x1, Pallas kernels, shards(): call(prepare, [fine, fine, fine, own], [HBM, HBM, VM], [dma((2,))], flops...  2.24 us
  transfers between devices with their start and end apart: 12, of which 6 were waited for; matrix products, arithmetic and copies ran while one was open for 0% of the time, Pallas kernels for 3%

profile of v1, /device:TPU:1, one launch (start us, length us, event | category | flops | bytes accessed | tf_op | source)
XLA Modules:
  0.0 86.1 jit_solution(11682665773698612794)
XLA Ops:
  0.0 2.5 %pack_fine.1 = (f32[1040,128]{1,0:T(8,128)S(1)}, f32[1040,128]{1,0:T(8,128)S(1)}, f32[13,64,128]{2,1,0:T(8,128)S(1)}, f32[13,64,128]{2,1,0:T(8,128)S(1)}, f32[64...) custom-call(f32[64,64,128]{2,1,0:T(8,128)} %load.3, f32[64,64,128]{2,1,0:T(8,128)} %start.3, f32[64,64,128]{2,1,0:T(8,128)} %mass_hbm.1), custom_call_target="tpu_custom_call" | custom-call | flops 1000000 | bytes 8000000 | tf_op jit(solution)/shard_map/pack_fine/pallas_call | solution.py:497
  2.5 2.1 %collective-permute-start = (f32[1040,128]{1,0:T(8,128)S(1)}, f32[1040,128]{1,0:T(8,128)S(1)}, u32[]{:S(2)}, u32[]{:S(2)}) collective-permute-start(f32[1040,128]{1,0:T(8,128)S(1)} %get-tuple-element.35), channel_id=1, source_target_pairs={{0,1},{1,0},{2,3},{3,2},{4,5},{5,4},{6,7},{7,6},{8,9},{9,8},{10,11... | collective-permute-start | bytes 1597448 | tf_op jit(solution)/shard_map/ppermute | solution.py:480
  4.6 10.9 %collective-permute-start.1 = (f32[1040,128]{1,0:T(8,128)S(1)}, f32[1040,128]{1,0:T(8,128)S(1)}, u32[]{:S(2)}, u32[]{:S(2)}) collective-permute-start(f32[1040,128]{1,0:T(8,128)S(1)} %get-tuple-element.36), channel_id=1, source_target_pairs={{0,31},{1,2},{2,1},{3,4},{4,3},{5,6},{6,5},{7,8},{8,7},{9,10},{10,... | collective-permute-start | bytes 1597448 | tf_op jit(solution)/shard_map/ppermute | solution.py:485
  15.5 1.2 %collective-permute-start.2 = (f32[13,64,128]{2,1,0:T(8,128)S(1)}, f32[13,64,128]{2,1,0:T(8,128)S(1)}, u32[]{:S(2)}, u32[]{:S(2)}) collective-permute-start(f32[13,64,128]{2,1,0:T(8,128)S(1)} %get-tuple-element.37), channel_id=1, source_target_pairs={{0,32},{32,0},{64,96},{96,64},{128,160},{160,128},{192,224},{224,1... | collective-permute-start | bytes 1277960 | tf_op jit(solution)/shard_map/ppermute | solution.py:480
  16.8 0.6 collective-permute-start.3
  17.4 0.0 collective-permute-done.m_even.re
  17.4 18.6 %collective-permute-done.1.m_odd.ro = f32[1040,128]{1,0:T(8,128)S(1)} collective-permute-done((f32[1040,128]{1,0:T(8,128)S(1)}, f32[1040,128]{1,0:T(8,128)S(1)}, u32[]{:S(2)}, u32[]{:S(2)}) %collective-permute-start.1) | collective-permute-done | bytes 532512 | tf_op jit(solution)/shard_map/ppermute | solution.py:485
  36.0 4.7 %collective-permute-start.4 = (f32[104,128]{1,0:T(8,128)S(1)}, f32[104,128]{1,0:T(8,128)S(1)}, u32[]{:S(2)}, u32[]{:S(2)}) collective-permute-start(f32[104,128]{1,0:T(8,128)S(1)} %get-tuple-element.39), channel_id=1, source_target_pairs={{0,32},{32,0},{64,96},{96,64},{128,160},{160,128},{192,224},{224,1... | collective-permute-start | bytes 159752 | tf_op jit(solution)/shard_map/ppermute | solution.py:480
  40.8 0.7 collective-permute-start.5
  41.4 2.2 %prepare.1 = (f32[74,80,128]{2,1,0:T(8,128)S(1)}, f32[74,80,128]{2,1,0:T(8,128)S(1)}, f32[74,80,128]{2,1,0:T(8,128)S(1)}, f32[64,64,128]{2,1,0:T(8,128)S(1)}) custom-call(f32[64,64,128]{2,1,0:T(8,128)} %load.3, f32[64,64,128]{2,1,0:T(8,128)} %start.3, f32[64,64,128]{2,1,0:T(8,128)S(1)} %get-tuple-element.29.mass), custom_call_target="tpu_custom_call" | custom-call | flops 100000000 | bytes 8000000 | tf_op jit(solution)/shard_map/prepare/pallas_call | solution.py:507
  43.7 0.0 collective-permute-done.2.be
  43.7 6.0 %collective-permute-done.3.bo = f32[13,64,128]{2,1,0:T(8,128)S(1)} collective-permute-done((f32[13,64,128]{2,1,0:T(8,128)S(1)}, f32[13,64,128]{2,1,0:T(8,128)S(1)}, u32[]{:S(2)}, u32[]{:S(2)}) %collective-permute-start.3) | collective-permute-done | bytes 426016 | tf_op jit(solution)/shard_map/ppermute | solution.py:485
  49.7 0.0 collective-permute-done.4.ce
  49.7 0.6 collective-permute-done.5.co
  50.3 5.0 %before.1 = (f32[74,80,128]{2,1,0:T(8,128)S(1)}, f32[74,80,128]{2,1,0:T(8,128)S(1)}, f32[74,80,128]{2,1,0:T(8,128)S(1)}, f32[42,48,128]{2,1,0:T(8,128)S(1)}, f32...) custom-call(f32[74,80,128]{2,1,0:T(8,128)S(1)} %get-tuple-element.30, ...), custom_call_target="tpu_custom_call", output_to_operand_aliasing={{1}: (1, {}), {2}: (2, {})} | custom-call | flops 100000000 | bytes 8000000 | tf_op jit(solution)/shard_map/before/pallas_call | solution.py:519
  55.3 0.1 collective-permute-start.8
  55.4 4.5 %collective-permute-start.9 = (f32[208,128]{1,0:T(8,128)S(1)}, f32[208,128]{1,0:T(8,128)S(1)}, u32[]{:S(2)}, u32[]{:S(2)}) collective-permute-start(f32[208,128]{1,0:T(8,128)S(1)} %get-tuple-element.49), channel_id=1, source_target_pairs={{0,31},{1,2},{2,1},{3,4},{4,3},{5,6},{6,5},{7,8},{8,7},{9,10},{10,... | collective-permute-start | bytes 319496 | tf_op jit(solution)/shard_map/ppermute | solution.py:485
  59.8 2.2 %collective-permute-start.6 = (f32[392,128]{1,0:T(8,128)S(1)}, f32[392,128]{1,0:T(8,128)S(1)}, u32[]{:S(2)}, u32[]{:S(2)}) collective-permute-start(f32[392,128]{1,0:T(8,128)S(1)} %get-tuple-element.45), channel_id=1, source_target_pairs={{0,32},{32,0},{64,96},{96,64},{128,160},{160,128},{192,224},{224,1... | collective-permute-start | bytes 602120 | tf_op jit(solution)/shard_map/ppermute | solution.py:480
  62.0 0.0 collective-permute-start.7
  62.0 0.0 collective-permute-done.8.re
  62.0 9.0 %collective-permute-done.9.ro = f32[208,128]{1,0:T(8,128)S(1)} collective-permute-done((f32[208,128]{1,0:T(8,128)S(1)}, f32[208,128]{1,0:T(8,128)S(1)}, u32[]{:S(2)}, u32[]{:S(2)}) %collective-permute-start.9) | collective-permute-done | bytes 106528 | tf_op jit(solution)/shard_map/ppermute | solution.py:485
  71.0 0.1 coarse_bands.1
  71.1 0.5 collective-permute-start.10
  71.6 0.0 collective-permute-start.11
  71.6 0.0 collective-permute-done.6.mbe
  71.6 0.0 collective-permute-done.7.mbo
  71.6 0.4 coarse_weights.1.mext
  72.0 0.7 collective-permute-done.10.lbe
  72.6 6.2 %collective-permute-done.11.lbo = f32[392,128]{1,0:T(8,128)S(1)} collective-permute-done((f32[392,128]{1,0:T(8,128)S(1)}, f32[392,128]{1,0:T(8,128)S(1)}, u32[]{:S(2)}, u32[]{:S(2)}) %collective-permute-start.11) | collective-permute-done | bytes 200736 | tf_op jit(solution)/shard_map/ppermute | solution.py:485
  78.8 7.3 %after.1 = f32[64,64,128]{2,1,0:T(8,128)} custom-call(f32[74,80,128]{2,1,0:T(8,128)S(1)} %get-tuple-element.41.v, f32[74,80,128]{2,1,0:T(8,128)S(1)} %get-tuple-element.42.f, f32[74,80,128]{2,1,0:T(8,128)S(1)} %get-tuple-element.43.w, f32[42,48,128]{2,1,0:T(8,128)S(1)} %coarse_weights.1.mext, f32[42,48,128]{2,1,0:T(8,128)S(1)} %get-tuple-element.50.lext_in, ...), custom_call_target="tpu_custom_call" | custom-call | flops 100000000 | bytes 8000000 | tf_op jit(solution)/shard_map/after/pallas_call | solution.py:539
  (1 shorter events, 0.0 us)
Async XLA Ops:
  2.5 14.9 %collective-permute-start = (f32[1040,128]{1,0:T(8,128)S(1)}, f32[1040,128]{1,0:T(8,128)S(1)}, u32[]{:S(2)}, u32[]{:S(2)}) collective-permute-start(f32[1040,128]{1,0:T(8,128)S(1)} %get-tuple-element.35), channel_id=1, source_target_pairs={{0,1},{1,0},{2,3},{3,2},{4,5},{5,4},{6,7},{7,6},{8,9},{9,8},{10,11... | collective-permute-start | bytes 1597448 | tf_op jit(solution)/shard_map/ppermute | solution.py:480
  4.6 31.4 %collective-permute-start.1 = (f32[1040,128]{1,0:T(8,128)S(1)}, f32[1040,128]{1,0:T(8,128)S(1)}, u32[]{:S(2)}, u32[]{:S(2)}) collective-permute-start(f32[1040,128]{1,0:T(8,128)S(1)} %get-tuple-element.36), channel_id=1, source_target_pairs={{0,31},{1,2},{2,1},{3,4},{4,3},{5,6},{6,5},{7,8},{8,7},{9,10},{10,... | collective-permute-start | bytes 1597448 | tf_op jit(solution)/shard_map/ppermute | solution.py:485
  15.5 28.2 %collective-permute-start.2 = (f32[13,64,128]{2,1,0:T(8,128)S(1)}, f32[13,64,128]{2,1,0:T(8,128)S(1)}, u32[]{:S(2)}, u32[]{:S(2)}) collective-permute-start(f32[13,64,128]{2,1,0:T(8,128)S(1)} %get-tuple-element.37), channel_id=1, source_target_pairs={{0,32},{32,0},{64,96},{96,64},{128,160},{160,128},{192,224},{224,1... | collective-permute-start | bytes 1277960 | tf_op jit(solution)/shard_map/ppermute | solution.py:480
  16.8 32.9 %collective-permute-start.3 = (f32[13,64,128]{2,1,0:T(8,128)S(1)}, f32[13,64,128]{2,1,0:T(8,128)S(1)}, u32[]{:S(2)}, u32[]{:S(2)}) collective-permute-start(f32[13,64,128]{2,1,0:T(8,128)S(1)} %get-tuple-element.38), channel_id=1, source_target_pairs={{0,224},{32,64},{64,32},{96,128},{128,96},{160,192},{192,160},{224... | collective-permute-start | bytes 1277960 | tf_op jit(solution)/shard_map/ppermute | solution.py:485
  36.0 13.7 %collective-permute-start.4 = (f32[104,128]{1,0:T(8,128)S(1)}, f32[104,128]{1,0:T(8,128)S(1)}, u32[]{:S(2)}, u32[]{:S(2)}) collective-permute-start(f32[104,128]{1,0:T(8,128)S(1)} %get-tuple-element.39), channel_id=1, source_target_pairs={{0,32},{32,0},{64,96},{96,64},{128,160},{160,128},{192,224},{224,1... | collective-permute-start | bytes 159752 | tf_op jit(solution)/shard_map/ppermute | solution.py:480
  40.8 9.5 %collective-permute-start.5 = (f32[104,128]{1,0:T(8,128)S(1)}, f32[104,128]{1,0:T(8,128)S(1)}, u32[]{:S(2)}, u32[]{:S(2)}) collective-permute-start(f32[104,128]{1,0:T(8,128)S(1)} %get-tuple-element.40), channel_id=1, source_target_pairs={{0,224},{32,64},{64,32},{96,128},{128,96},{160,192},{192,160},{224... | collective-permute-start | bytes 159752 | tf_op jit(solution)/shard_map/ppermute | solution.py:485
  55.3 6.8 %collective-permute-start.8 = (f32[208,128]{1,0:T(8,128)S(1)}, f32[208,128]{1,0:T(8,128)S(1)}, u32[]{:S(2)}, u32[]{:S(2)}) collective-permute-start(f32[208,128]{1,0:T(8,128)S(1)} %get-tuple-element.48), channel_id=1, source_target_pairs={{0,1},{1,0},{2,3},{3,2},{4,5},{5,4},{6,7},{7,6},{8,9},{9,8},{10,11... | collective-permute-start | bytes 319496 | tf_op jit(solution)/shard_map/ppermute | solution.py:480
  55.4 15.6 %collective-permute-start.9 = (f32[208,128]{1,0:T(8,128)S(1)}, f32[208,128]{1,0:T(8,128)S(1)}, u32[]{:S(2)}, u32[]{:S(2)}) collective-permute-start(f32[208,128]{1,0:T(8,128)S(1)} %get-tuple-element.49), channel_id=1, source_target_pairs={{0,31},{1,2},{2,1},{3,4},{4,3},{5,6},{6,5},{7,8},{8,7},{9,10},{10,... | collective-permute-start | bytes 319496 | tf_op jit(solution)/shard_map/ppermute | solution.py:485
  59.8 11.7 %collective-permute-start.6 = (f32[392,128]{1,0:T(8,128)S(1)}, f32[392,128]{1,0:T(8,128)S(1)}, u32[]{:S(2)}, u32[]{:S(2)}) collective-permute-start(f32[392,128]{1,0:T(8,128)S(1)} %get-tuple-element.45), channel_id=1, source_target_pairs={{0,32},{32,0},{64,96},{96,64},{128,160},{160,128},{192,224},{224,1... | collective-permute-start | bytes 602120 | tf_op jit(solution)/shard_map/ppermute | solution.py:480
  62.0 9.5 %collective-permute-start.7 = (f32[392,128]{1,0:T(8,128)S(1)}, f32[392,128]{1,0:T(8,128)S(1)}, u32[]{:S(2)}, u32[]{:S(2)}) collective-permute-start(f32[392,128]{1,0:T(8,128)S(1)} %get-tuple-element.46), channel_id=1, source_target_pairs={{0,224},{32,64},{64,32},{96,128},{128,96},{160,192},{192,160},{224... | collective-permute-start | bytes 602120 | tf_op jit(solution)/shard_map/ppermute | solution.py:485
  71.1 1.6 %collective-permute-start.10 = (f32[392,128]{1,0:T(8,128)S(1)}, f32[392,128]{1,0:T(8,128)S(1)}, u32[]{:S(2)}, u32[]{:S(2)}) collective-permute-start(f32[392,128]{1,0:T(8,128)S(1)} %get-tuple-element.51), channel_id=1, source_target_pairs={{0,32},{32,0},{64,96},{96,64},{128,160},{160,128},{192,224},{224,1... | collective-permute-start | bytes 602120 | tf_op jit(solution)/shard_map/ppermute | solution.py:480
  71.6 7.2 %collective-permute-start.11 = (f32[392,128]{1,0:T(8,128)S(1)}, f32[392,128]{1,0:T(8,128)S(1)}, u32[]{:S(2)}, u32[]{:S(2)}) collective-permute-start(f32[392,128]{1,0:T(8,128)S(1)} %get-tuple-element.52), channel_id=1, source_target_pairs={{0,224},{32,64},{64,32},{96,128},{128,96},{160,192},{192,160},{224... | collective-permute-start | bytes 602120 | tf_op jit(solution)/shard_map/ppermute | solution.py:485
